TPU v7x, 32 devices: a whole 2x2x4 slice. The times are simulated.
32 devices in a mesh: rows: 8 (over z, x), rep: 4 (over y, core).
Axes of the slice: x: 2, y: 2, z: 4, core: 2. Of those that a mesh axis runs over, the one named last changes fastest.
Arguments:
- requests: int32 [32, 8, 128], P(('rows', 'rep')), may hold values from 0 to 1023
- request_counts: int32 [32, 8], P(('rows', 'rep')), may hold values from 0 to 128, as said below
- table: bfloat16 [8192, 512], P('rows')
- gain: float32 [512], replicated, may hold values from 0.5 to 1.5
Outputs:
- normalized: bfloat16 [32, 8, 128, 512], P(('rows', 'rep'))
- row_counts: int32 [8192], P('rows')
- moments: float32 [2, 2], replicated
Inputs may be any that keep to these rules, and one draw needn't show every extreme that they name: Each device uses request_counts[d, o] of its 128 slots toward owner o; in every draw one owner's slots are full from every device.
All inputs are finite; a program needn't handle non-finite values.
Results may differ from a plain program's by a relative error of at most 0.0004.
Values may be sent and summed in bfloat16 or wider, within the bound.
No kernel may reach another device: no remote copies, remote signals or barrier semaphores. Data moves between devices by JAX's collectives and lax.ppermute only.
A program may use at most 64 MiB of HBM per device.

v0:
```python
import jax
import jax.numpy as jnp
from jax import lax
from jax.sharding import PartitionSpec as P

WIDTH = 256
LAYERS = 2
epsilon = 1e-06


def joined(part, axis, combine):
    gathered = jax.tree.map(lambda a: lax.all_gather(a, axis), part)

    def take(source):
        return jax.tree.map(lambda a: lax.dynamic_index_in_dim(a, source, 0, False), gathered)

    return lax.fori_loop(
        1, lax.axis_size(axis), lambda source, state: combine(state, take(source)), take(0)
    )


def merge_moments(former, latter):
    count_former, mean_former, square_former = former
    count_latter, mean_latter, square_latter = latter
    merged_count = count_former + count_latter
    safe_count = jnp.maximum(merged_count, 1.0)
    delta_mean = mean_latter - mean_former
    merged_mean = mean_former + delta_mean * count_latter / safe_count
    merged_square = (
        square_former
        + square_latter
        + delta_mean * delta_mean * count_former * count_latter / safe_count
    )
    return (merged_count, merged_mean, merged_square)


def per_device(requests, request_counts, table, gain):
    wanted, wanted_counts = (
        lax.all_to_all(requests, "rows", split_axis=1, concat_axis=0, tiled=True),
        lax.all_to_all(request_counts, "rows", split_axis=1, concat_axis=0, tiled=True),
    )
    owners = wanted.shape[0]
    slot_count = wanted.shape[2]
    held_rows = table.shape[0]
    row_index = wanted.reshape(-1)
    live_slot = lax.broadcasted_iota(jnp.int32, (owners, slot_count), 1) < wanted_counts
    live_flat = live_slot.reshape(-1)
    matches = (row_index[:, None] == jnp.arange(held_rows, dtype=jnp.int32)[None, :]) & live_flat[
        :, None
    ]
    local_counts = jnp.sum(matches.astype(jnp.int32), axis=0)
    row_counts = lax.psum(local_counts, "rep")
    shaped = table.reshape(held_rows, LAYERS, WIDTH)
    weights = row_counts.astype(jnp.float32)
    partial_value = jnp.dot(
        weights, jnp.sum(shaped, axis=2, dtype=jnp.float32), precision=lax.Precision.HIGHEST
    )
    count_layers = jnp.full((LAYERS,), jnp.sum(weights) * WIDTH, jnp.float32)
    mean_here = partial_value / jnp.maximum(count_layers, 1.0)
    centered = jnp.sum(jnp.square(shaped.astype(jnp.float32) - mean_here[None, :, None]), axis=2)
    square_here = jnp.dot(weights, centered, precision=lax.Precision.HIGHEST)
    entries, layer_mean, merged_square = joined(
        (count_layers, mean_here, square_here), "rows", merge_moments
    )
    layer_var = merged_square / entries
    inverse = jnp.repeat(lax.rsqrt(layer_var + epsilon), WIDTH) * gain
    mean_full = jnp.repeat(layer_mean, WIDTH)
    looked = jnp.take(table, row_index, axis=0).reshape(owners, 1, slot_count, LAYERS * WIDTH)
    scaled = (looked.astype(jnp.float32) - mean_full) * inverse
    scaled = jnp.where(live_slot.reshape(owners, 1, slot_count, 1), scaled, 0.0).astype(
        jnp.bfloat16
    )
    normalized = lax.all_to_all(scaled, "rows", split_axis=0, concat_axis=1, tiled=True)
    return (normalized, row_counts, jnp.stack([layer_mean, layer_var]))


def solution(mesh):
    return jax.shard_map(
        per_device,
        mesh=mesh,
        in_specs=(P(("rows", "rep"), None, None), P(("rows", "rep"), None), P("rows", None), P()),
        out_specs=(P(("rows", "rep"), None, None, None), P("rows"), P()),
        check_vma=False,
    )
```

profile of v0, /device:TPU:0, one launch (start us, length us, event | category | flops | bytes accessed | tf_op | source)
XLA Modules:
  0.0 89.4 jit_solution(5345991908360352691)
XLA Ops:
  0.6 1.3 %copy.13 = s32[1,8,1]{2,0,1:T(1,128)} copy(s32[1,8,1]{1,2,0:T(1,128)} %bitcast.86) | data formatting | bytes 64 | tf_op jit(solution)/shard_map/all_to_all | solution.py:40
  2.0 7.3 %all-to-all-start = ((s32[1,8,1]{2,0,1:T(1,128)}), s32[1,8,1]{2,0,1:T(1,128)S(1)}, u32[]{:S(2)}, u32[]{:S(2)}) async-start(s32[1,8,1]{2,0,1:T(1,128)} %copy.13), calls=%async_computation | async-start | bytes 8192 | tf_op jit(solution)/shard_map/all_to_all | solution.py:40
  9.2 2.4 %reshape.157 = f32[1024,2,256]{2,1,0:T(2,128)S(1)} reshape(bf16[1024,512]{1,0:T(8,128)(2,1)} %param.8) | data formatting | bytes 3145728 | tf_op jit(solution)/shard_map/convert_element_type | solution.py:56
  11.6 1.9 %reduce_sum.38 = f32[1024,2]{1,0:T(8,128)} reduce(f32[1024,2,256]{2,1,0:T(2,128)S(1)} %reshape.157, f32[]{:T(128)} %constant.79.clone.1), dimensions={2}, to_apply=%region_3.0 | reduce | flops 522240 | bytes 2105348 | tf_op jit(solution)/shard_map/reduce_sum | solution.py:56
  13.6 0.7 dynamic-slice
  14.9 0.7 all-to-all-done
  15.7 5.3 %all-to-all-start.1 = ((s32[1,8,128]{2,0,1:T(1,128)}), s32[1,8,128]{2,0,1:T(1,128)S(1)}, u32[]{:S(2)}, u32[]{:S(2)}) async-start(s32[1,8,128]{2,0,1:T(1,128)} %bitcast.4), calls=%async_computation.1 | async-start | bytes 8192 | tf_op jit(solution)/shard_map/all_to_all | solution.py:39
  21.3 6.1 %all-to-all-done.1 = s32[1,8,128]{2,0,1:T(1,128)S(1)} async-done(((s32[1,8,128]{2,0,1:T(1,128)}), s32[1,8,128]{2,0,1:T(1,128)S(1)}, u32[]{:S(2)}, u32[]{:S(2)}) %all-to-all-start.1) | async-done | bytes 4128 | tf_op jit(solution)/shard_map/all_to_all | solution.py:39
  27.4 0.8 convert_reduce_fusion
  28.1 5.0 %psum.7 = s32[1024]{0:T(1024)S(1)} all-reduce(s32[1024]{0:T(1024)S(1)} %convert_reduce_fusion), channel_id=1, replica_groups=mesh['rows'=8,'rep'=4] {'rep'}, use_global_device_ids=true, to_apply=%region_1.0 | all-reduce | flops 1024 | bytes 8192 | tf_op jit(solution)/shard_map/psum | solution.py:52
  33.1 0.6 convert_reduce_fusion.1
  34.4 1.4 %fusion.8 = f32[2]{0:T(128)S(1)} fusion(f32[1024,1]{0,1:T(1,128)S(1)} %bitcast.77, f32[1024,2]{1,0:T(8,128)} %reduce_sum.38, f32[]{:T(128)S(6)} %max.14), kind=kOutput, calls=%fused_computation.19 | convolution fusion | flops 24578 | bytes 12300 | tf_op jit(solution)/shard_map/dot_general | solution.py:55
  35.8 1.3 %multiply_reduce_fusion = f32[1024,2]{1,0:T(8,128)S(1)} fusion(f32[1024,2,256]{2,1,0:T(2,128)S(1)} %reshape.157, f32[2]{0:T(128)S(1)} %fusion.8), kind=kLoop, calls=%fused_computation.16 | loop fusion | flops 1570816 | bytes 2105352 | tf_op jit(solution)/shard_map/reduce_sum | solution.py:60
  37.0 0.4 convolution_bitcast_fusion
  37.4 0.2 dynamic-update-slice.1
  37.8 0.8 dynamic-update-slice
  38.6 17.7 %all-reduce.3 = (f32[8]{0:T(128)S(1)}, f32[16]{0:T(128)S(1)}, f32[16]{0:T(128)S(1)}) all-reduce(f32[8]{0:T(128)S(1)} %dynamic-update-slice, f32[16]{0:T(128)S(1)} %dynamic-update-slice.1, f32[16]{0:T(128)S(1)} %dynamic-update-slice.2), channel_id=2, replica_groups=mesh['rows'=8,'rep'=4] {'rows'}, use_global_device_ids=true, to_apply=%add | all-reduce | flops 40 | bytes 320
  56.6 0.5 while.19
  57.3 4.0 %gather_fusion = bf16[1024,512]{1,0:T(8,128)(2,1)S(1)} fusion(bf16[1024,512]{1,0:T(8,128)(2,1)S(1)} %copy-done, s32[1024]{0:T(1024)S(1)} %broadcast_clamp_fusion), kind=kCustom, calls=%fused_computation | custom fusion | bytes 2101248 | tf_op jit(solution)/shard_map/jit(_take)/gather | solution.py:68
  61.3 1.8 %select_convert_fusion = bf16[8,1,128,512]{3,2,1,0:T(8,128)(2,1)} fusion(f32[512]{0:T(512)S(1)} %mul.63, f32[512]{0:T(512)S(1)} %bitcast.83, bf16[8,1,128,512]{3,2,1,0:T(8,128)(2,1)S(1)} %bitcast.73, pred[8,128]{1,0:T(8,128)(4,1)S(1)} %compare_and_fusion, pred[8,128]{1,0:T(8,128)(4,1)S(1)} %get-tuple-element.205), kind=kLoop, calls=%fused_computation.15 | loop fusion | flops 3145728 | bytes 2103296 | tf_op jit(solution)/shard_map/convert_element_type | solution.py:70
  63.1 3.6 %all-to-all-start.2 = ((bf16[8,1,128,512]{3,2,1,0:T(8,128)(2,1)}), bf16[8,1,128,512]{3,2,1,0:T(8,128)(2,1)S(1)}, u32[]{:S(2)}, u32[]{:S(2)}) async-start(bf16[8,1,128,512]{3,2,1,0:T(8,128)(2,1)} %select_convert_fusion), calls=%async_computation.2 | async-start | bytes 2097152 | tf_op jit(solution)/shard_map/all_to_all | solution.py:73
  66.6 0.6 pad_maximum_fusion
  67.2 21.2 %all-to-all-done.2 = bf16[8,1,128,512]{3,2,1,0:T(8,128)(2,1)S(1)} async-done(((bf16[8,1,128,512]{3,2,1,0:T(8,128)(2,1)}), bf16[8,1,128,512]{3,2,1,0:T(8,128)(2,1)S(1)}, u32[]{:S(2)}, u32[]{:S(2)}) %all-to-all-start.2) | async-done | bytes 1048608 | tf_op jit(solution)/shard_map/all_to_all | solution.py:73
  88.4 1.0 %copy.35 = bf16[1,8,128,512]{3,2,1,0:T(8,128)(2,1)} copy(bf16[1,8,128,512]{3,2,1,0:T(8,128)(2,1)S(1)} %bitcast.74) | data formatting | bytes 2097152
  (42 shorter events, 1.3 us)
Async XLA Ops:
  2.0 13.7 %all-to-all-start = ((s32[1,8,1]{2,0,1:T(1,128)}), s32[1,8,1]{2,0,1:T(1,128)S(1)}, u32[]{:S(2)}, u32[]{:S(2)}) async-start(s32[1,8,1]{2,0,1:T(1,128)} %copy.13), calls=%async_computation | async-start | bytes 8192 | tf_op jit(solution)/shard_map/all_to_all | solution.py:40
  11.6 2.0 %copy-start.3 = (u32[32]{0:T(128)S(1)}, u32[32]{0:T(128)}, u32[]{:S(2)}) copy-start(u32[32]{0:T(128)} %constant.87) | copy-start | bytes 388
  13.6 43.7 %copy-start = (bf16[1024,512]{1,0:T(8,128)(2,1)S(1)}, bf16[1024,512]{1,0:T(8,128)(2,1)}, u32[]{:S(2)}) copy-start(bf16[1024,512]{1,0:T(8,128)(2,1)} %param.8) | copy-start | bytes 3145732
  15.7 11.7 %all-to-all-start.1 = ((s32[1,8,128]{2,0,1:T(1,128)}), s32[1,8,128]{2,0,1:T(1,128)S(1)}, u32[]{:S(2)}, u32[]{:S(2)}) async-start(s32[1,8,128]{2,0,1:T(1,128)} %bitcast.4), calls=%async_computation.1 | async-start | bytes 8192 | tf_op jit(solution)/shard_map/all_to_all | solution.py:39
  33.1 28.2 %copy-start.1 = (s32[1024]{0:T(1024)}, s32[1024]{0:T(1024)S(1)}, u32[]{:S(2)}) copy-start(s32[1024]{0:T(1024)S(1)} %psum.7) | copy-start | bytes 12292
  57.3 4.0 %copy-start.2 = (f32[512]{0:T(512)S(1)}, f32[512]{0:T(512)}, u32[]{:S(2)}) copy-start(f32[512]{0:T(512)} %param.9) | copy-start | bytes 6148
  63.1 25.4 %all-to-all-start.2 = ((bf16[8,1,128,512]{3,2,1,0:T(8,128)(2,1)}), bf16[8,1,128,512]{3,2,1,0:T(8,128)(2,1)S(1)}, u32[]{:S(2)}, u32[]{:S(2)}) async-start(bf16[8,1,128,512]{3,2,1,0:T(8,128)(2,1)} %select_convert_fusion), calls=%async_computation.2 | async-start | bytes 2097152 | tf_op jit(solution)/shard_map/all_to_all | solution.py:73
where the time goes:
time: 89.8 us; the launch traced here: 89.4 us
  waiting for transfers between devices  28.1 us (31%)
  blocking collectives  22.6 us (25%)
  starting transfers between devices  16.1 us (18%)
  local copies, waits for them, and re-layouts  11 us (12%)
  other arithmetic  7.57 us (8%)
  between operations  2.13 us (2%)
  matrix products  1.75 us (2%)
    all_to_all x1, waiting for transfers between devices, per_device(): lax.all_to_all(scaled, 'rows', split_axis=0, concat_axis=1, tiled=True)  21.2 us
    unnamed x1, blocking collectives  17.7 us
    all_to_all x1, starting transfers between devices, per_device(): lax.all_to_all(request_counts, 'rows', split_axis=1, concat_axis=0, tiled...  7.28 us
    all_to_all x1, waiting for transfers between devices, per_device(): lax.all_to_all(requests, 'rows', split_axis=1, concat_axis=0, tiled=True)  6.11 us
    all_to_all x1, starting transfers between devices, per_device(): lax.all_to_all(requests, 'rows', split_axis=1, concat_axis=0, tiled=True)  5.29 us
    psum x1, blocking collectives, per_device(): row_counts = lax.psum(local_counts, 'rep')  4.97 us
    gather x1, local copies, waits for them, and re-layouts, per_device(): jnp.take(table, row_index, axis=0)  3.97 us
    all_to_all x1, starting transfers between devices, per_device(): lax.all_to_all(scaled, 'rows', split_axis=0, concat_axis=1, tiled=True)  3.56 us
  transfers between devices with their start and end apart: 3, of which 3 were waited for; matrix products, arithmetic and copies ran while one was open for 7% of the time, Pallas kernels for 0%

commit v1 on v0

--- a/solution.py
+++ b/solution.py
@@ -70,7 +70,10 @@
     scaled = jnp.where(live_slot.reshape(owners, 1, slot_count, 1), scaled, 0.0).astype(
         jnp.bfloat16
     )
-    normalized = lax.all_to_all(scaled, "rows", split_axis=0, concat_axis=1, tiled=True)
+    normalized = jnp.concatenate(
+        lax.all_to_all(jnp.stack(jnp.split(scaled, lax.axis_size("rows"), axis=0)), "rows", 0, 0),
+        axis=1,
+    )
     return (normalized, row_counts, jnp.stack([layer_mean, layer_var]))
 
 

time: 89.8 us -> 94.3 us (1.050)
  local copies, waits for them, and re-layouts: 11 us -> 16.3 us
    unnamed x21 -> x28, local copies, waits for them, and re-layouts: 3.12 us -> 7.77 us
  transfers between devices with their start and end apart: 3 -> 3, of which waited for: 3 -> 3; matrix products, arithmetic and copies ran while one was open for 7% -> 6% of each run, Pallas kernels for 0% -> 0%
where the time goes in v1:
time: 94.3 us; the launch traced here: 93.9 us
  waiting for transfers between devices  28.1 us (30%)
  blocking collectives  22.6 us (24%)
  local copies, waits for them, and re-layouts  16.3 us (17%)
  starting transfers between devices  16.1 us (17%)
  other arithmetic  6.78 us (7%)
  between operations  2.14 us (2%)
  matrix products  1.75 us (2%)
    all_to_all x1, waiting for transfers between devices, per_device(): lax.all_to_all(jnp.stack(jnp.split(scaled, lax.axis_size('rows'), axis=0)...  21.2 us
    unnamed x1, blocking collectives  17.7 us
    unnamed x28, local copies, waits for them, and re-layouts  7.77 us
    all_to_all x1, starting transfers between devices, per_device(): lax.all_to_all(request_counts, 'rows', split_axis=1, concat_axis=0, tiled...  7.28 us
    all_to_all x1, waiting for transfers between devices, per_device(): lax.all_to_all(requests, 'rows', split_axis=1, concat_axis=0, tiled=True)  6.11 us
    all_to_all x1, starting transfers between devices, per_device(): lax.all_to_all(requests, 'rows', split_axis=1, concat_axis=0, tiled=True)  5.29 us
    psum x1, blocking collectives, per_device(): row_counts = lax.psum(local_counts, 'rep')  4.97 us
    gather x1, local copies, waits for them, and re-layouts, per_device(): jnp.take(table, row_index, axis=0)  3.97 us
  transfers between devices with their start and end apart: 3, of which 3 were waited for; matrix products, arithmetic and copies ran while one was open for 6% of the time, Pallas kernels for 0%

profile of v1, /device:TPU:0, one launch (start us, length us, event | category | flops | bytes accessed | tf_op | source)
XLA Modules:
  0.0 93.9 jit_solution(3397284827078001502)
XLA Ops:
  0.6 1.3 %copy.29 = s32[1,8,1]{2,0,1:T(1,128)} copy(s32[1,8,1]{1,2,0:T(1,128)} %bitcast.118) | data formatting | bytes 64 | tf_op jit(solution)/shard_map/all_to_all | solution.py:40
  2.0 7.3 %all-to-all-start = ((s32[1,8,1]{2,0,1:T(1,128)}), s32[1,8,1]{2,0,1:T(1,128)S(1)}, u32[]{:S(2)}, u32[]{:S(2)}) async-start(s32[1,8,1]{2,0,1:T(1,128)} %copy.29), calls=%async_computation | async-start | bytes 8192 | tf_op jit(solution)/shard_map/all_to_all | solution.py:40
  9.2 2.4 %reshape.158 = f32[1024,2,256]{2,1,0:T(2,128)S(1)} reshape(bf16[1024,512]{1,0:T(8,128)(2,1)} %param.8) | data formatting | bytes 3145728 | tf_op jit(solution)/shard_map/convert_element_type | solution.py:56
  11.6 1.9 %reduce_sum.38 = f32[1024,2]{1,0:T(8,128)} reduce(f32[1024,2,256]{2,1,0:T(2,128)S(1)} %reshape.158, f32[]{:T(128)} %constant.79.clone.1), dimensions={2}, to_apply=%region_3.0 | reduce | flops 522240 | bytes 2105348 | tf_op jit(solution)/shard_map/reduce_sum | solution.py:56
  14.9 0.7 all-to-all-done
  15.7 5.3 %all-to-all-start.1 = ((s32[1,8,128]{2,0,1:T(1,128)}), s32[1,8,128]{2,0,1:T(1,128)S(1)}, u32[]{:S(2)}, u32[]{:S(2)}) async-start(s32[1,8,128]{2,0,1:T(1,128)} %bitcast.4), calls=%async_computation.1 | async-start | bytes 8192 | tf_op jit(solution)/shard_map/all_to_all | solution.py:39
  21.3 6.1 %all-to-all-done.1 = s32[1,8,128]{2,0,1:T(1,128)S(1)} async-done(((s32[1,8,128]{2,0,1:T(1,128)}), s32[1,8,128]{2,0,1:T(1,128)S(1)}, u32[]{:S(2)}, u32[]{:S(2)}) %all-to-all-start.1) | async-done | bytes 4128 | tf_op jit(solution)/shard_map/all_to_all | solution.py:39
  27.4 0.8 convert_reduce_fusion
  28.1 5.0 %psum.7 = s32[1024]{0:T(1024)S(1)} all-reduce(s32[1024]{0:T(1024)S(1)} %convert_reduce_fusion), channel_id=1, replica_groups=mesh['rows'=8,'rep'=4] {'rep'}, use_global_device_ids=true, to_apply=%region_1.0 | all-reduce | flops 1024 | bytes 8192 | tf_op jit(solution)/shard_map/psum | solution.py:52
  34.4 1.4 %fusion.8 = f32[2]{0:T(128)S(1)} fusion(f32[1024,1]{0,1:T(1,128)S(1)} %bitcast.109, f32[1024,2]{1,0:T(8,128)} %reduce_sum.38, f32[]{:T(128)S(6)} %max.14), kind=kOutput, calls=%fused_computation.19 | convolution fusion | flops 24578 | bytes 12300 | tf_op jit(solution)/shard_map/dot_general | solution.py:55
  35.8 1.3 %multiply_reduce_fusion = f32[1024,2]{1,0:T(8,128)S(1)} fusion(f32[1024,2,256]{2,1,0:T(2,128)S(1)} %reshape.158, f32[2]{0:T(128)S(1)} %fusion.8), kind=kLoop, calls=%fused_computation.16 | loop fusion | flops 1570816 | bytes 2105352 | tf_op jit(solution)/shard_map/reduce_sum | solution.py:60
  37.8 0.8 dynamic-update-slice
  38.6 17.7 %all-reduce.3 = (f32[8]{0:T(128)S(1)}, f32[16]{0:T(128)S(1)}, f32[16]{0:T(128)S(1)}) all-reduce(f32[8]{0:T(128)S(1)} %dynamic-update-slice, f32[16]{0:T(128)S(1)} %dynamic-update-slice.1, f32[16]{0:T(128)S(1)} %dynamic-update-slice.2), channel_id=2, replica_groups=mesh['rows'=8,'rep'=4] {'rows'}, use_global_device_ids=true, to_apply=%add | all-reduce | flops 40 | bytes 320
  57.3 4.0 %gather_fusion = bf16[1024,512]{1,0:T(8,128)(2,1)S(1)} fusion(bf16[1024,512]{1,0:T(8,128)(2,1)S(1)} %copy-done, s32[1024]{0:T(1024)S(1)} %broadcast_clamp_fusion), kind=kCustom, calls=%fused_computation | custom fusion | bytes 2101248 | tf_op jit(solution)/shard_map/jit(_take)/gather | solution.py:68
  61.3 1.0 %select_convert_fusion = bf16[8,1,128,512]{3,2,1,0:T(8,128)(2,1)S(1)} fusion(f32[512]{0:T(512)S(1)} %mul.63, f32[512]{0:T(512)S(1)} %bitcast.115, bf16[8,1,128,512]{3,2,1,0:T(8,128)(2,1)S(1)} %bitcast.105, pred[8,128]{1,0:T(8,128)(4,1)S(1)} %compare_and_fusion, pred[8,128]{1,0:T(8,128)(4,1)S(1)} %get-tuple-element.205), kind=kLoop, calls=%fused_computation.15 | loop fusion | flops 3145728 | bytes 2103296 | tf_op jit(solution)/shard_map/convert_element_type | solution.py:70
  62.3 0.7 fusion.16
  62.9 0.7 fusion.15
  63.6 0.7 fusion.14
  64.3 0.7 fusion.13
  64.9 0.7 fusion.12
  65.6 0.7 fusion.11
  67.6 3.6 %all-to-all-start.2 = ((bf16[8,1,1,128,512]{4,3,2,1,0:T(8,128)(2,1)}), bf16[8,1,1,128,512]{4,3,2,1,0:T(8,128)(2,1)S(1)}, u32[]{:S(2)}, u32[]{:S(2)}) async-start(bf16[8,1,1,128,512]{4,3,2,1,0:T(8,128)(2,1)} %fusion.9), calls=%async_computation.2 | async-start | bytes 2097152 | tf_op jit(solution)/shard_map/all_to_all | solution.py:74
  71.7 21.2 %all-to-all-done.2 = bf16[8,1,1,128,512]{4,3,2,1,0:T(8,128)(2,1)S(1)} async-done(((bf16[8,1,1,128,512]{4,3,2,1,0:T(8,128)(2,1)}), bf16[8,1,1,128,512]{4,3,2,1,0:T(8,128)(2,1)S(1)}, u32[]{:S(2)}, u32[]{:S(2)}) %all-to-all-start.2) | async-done | bytes 1048608 | tf_op jit(solution)/shard_map/all_to_all | solution.py:74
  93.0 1.0 %copy.58 = bf16[1,8,128,512]{3,2,1,0:T(8,128)(2,1)} copy(bf16[1,8,128,512]{3,2,1,0:T(8,128)(2,1)S(1)} %bitcast.106) | data formatting | bytes 2097152
  (50 shorter events, 5.5 us)
Async XLA Ops:
  2.0 13.7 %all-to-all-start = ((s32[1,8,1]{2,0,1:T(1,128)}), s32[1,8,1]{2,0,1:T(1,128)S(1)}, u32[]{:S(2)}, u32[]{:S(2)}) async-start(s32[1,8,1]{2,0,1:T(1,128)} %copy.29), calls=%async_computation | async-start | bytes 8192 | tf_op jit(solution)/shard_map/all_to_all | solution.py:40
  11.6 2.0 %copy-start.3 = (u32[32]{0:T(128)S(1)}, u32[32]{0:T(128)}, u32[]{:S(2)}) copy-start(u32[32]{0:T(128)} %constant.87) | copy-start | bytes 388
  13.6 43.7 %copy-start = (bf16[1024,512]{1,0:T(8,128)(2,1)S(1)}, bf16[1024,512]{1,0:T(8,128)(2,1)}, u32[]{:S(2)}) copy-start(bf16[1024,512]{1,0:T(8,128)(2,1)} %param.8) | copy-start | bytes 3145732
  15.7 11.7 %all-to-all-start.1 = ((s32[1,8,128]{2,0,1:T(1,128)}), s32[1,8,128]{2,0,1:T(1,128)S(1)}, u32[]{:S(2)}, u32[]{:S(2)}) async-start(s32[1,8,128]{2,0,1:T(1,128)} %bitcast.4), calls=%async_computation.1 | async-start | bytes 8192 | tf_op jit(solution)/shard_map/all_to_all | solution.py:39
  33.1 28.2 %copy-start.1 = (s32[1024]{0:T(1024)}, s32[1024]{0:T(1024)S(1)}, u32[]{:S(2)}) copy-start(s32[1024]{0:T(1024)S(1)} %psum.7) | copy-start | bytes 12292
  57.3 4.0 %copy-start.2 = (f32[512]{0:T(512)S(1)}, f32[512]{0:T(512)}, u32[]{:S(2)}) copy-start(f32[512]{0:T(512)} %param.9) | copy-start | bytes 6148
  67.6 25.4 %all-to-all-start.2 = ((bf16[8,1,1,128,512]{4,3,2,1,0:T(8,128)(2,1)}), bf16[8,1,1,128,512]{4,3,2,1,0:T(8,128)(2,1)S(1)}, u32[]{:S(2)}, u32[]{:S(2)}) async-start(bf16[8,1,1,128,512]{4,3,2,1,0:T(8,128)(2,1)} %fusion.9), calls=%async_computation.2 | async-start | bytes 2097152 | tf_op jit(solution)/shard_map/all_to_all | solution.py:74
